TPU v7x, 128 devices: a whole 4x4x4 slice. The times are simulated.
128 devices in a mesh: band: 8 (over x, core), grid: 16 (over z, y).
Axes of the slice: x: 4, y: 4, z: 4, core: 2. Of those that a mesh axis runs over, the one named last changes fastest.
Arguments:
- orbitals: bfloat16 [32768, 2048], P('grid', 'band'), may hold values from -6 to 6
- projectors: bfloat16 [128, 8, 128], replicated, may hold values from -0.5 to 0.5
- sphere_start: int32 [128], replicated, may hold values from 0 to 1920, as said below
- proj_count: int32 [128], replicated, may hold values from 1 to 8
- owner_slab: int32 [128], replicated, may hold values from 0 to 15, as said below
- correlation_coef: float32 [128, 8, 8], replicated, as said below
Outputs:
- rotated: bfloat16 [32768, 2048], P(('grid', 'band'))
Inputs may be any that keep to these rules, and one draw needn't show every extreme that they name: `sphere_start`: a multiple of 128. `owner_slab`: every slab owns exactly 8 atoms. `correlation_coef`: each atom's matrix is symmetric positive definite.
All inputs are finite; a program needn't handle non-finite values.
Results may differ from a plain program's by a relative error of at most 0.0049.
Values may be sent and summed in bfloat16 or wider, within the bound.
A program may use at most 128 MiB of HBM per device.

v0:
```python
import jax
import jax.numpy as jnp
from jax import lax
from jax.sharding import PartitionSpec as P

SPH = 128
NPMAX = 8
A_SLAB = 8


def inverse_factor(matrix):
    order = matrix.shape[0]
    if order <= 512 or order % 2 != 0:
        lower = jnp.linalg.cholesky(matrix)
        identity = jnp.eye(order, dtype=matrix.dtype)
        return lax.linalg.triangular_solve(lower, identity, left_side=True, lower=True)
    half = order // 2
    upper_inv = inverse_factor(matrix[:half, :half])
    below = jnp.dot(matrix[half:, :half], upper_inv.T, precision=lax.Precision.HIGHEST)
    schur = matrix[half:, half:] - jnp.dot(below, below.T, precision=lax.Precision.HIGHEST)
    lower_inv = inverse_factor(schur)
    corner = -jnp.dot(
        lower_inv,
        jnp.dot(below, upper_inv, precision=lax.Precision.HIGHEST),
        precision=lax.Precision.HIGHEST,
    )
    top = jnp.concatenate([upper_inv, jnp.zeros((half, order - half), matrix.dtype)], axis=1)
    bottom = jnp.concatenate([corner, lower_inv], axis=1)
    return jnp.concatenate([top, bottom], axis=0)


def slab_atoms(owner_slab, slab):
    atoms = owner_slab.shape[0]
    keyed = jnp.where(owner_slab == slab, 0, 1) * atoms + jnp.arange(atoms, dtype=jnp.int32)
    return jnp.argsort(keyed, stable=True)[:A_SLAB]


def atom_terms(source, weights, starts, counts, coefs, valid):

    def take_rows(offset):
        return lax.dynamic_slice_in_dim(source, offset, SPH, 0)

    sphere_rows = jax.vmap(take_rows)(starts)
    correlations = jnp.einsum(
        "aij,ajn->ain", weights, sphere_rows, preferred_element_type=jnp.float32
    )
    active = (jnp.arange(NPMAX)[None, :] < counts[:, None]) & valid[:, None]
    correlations = jnp.where(active[:, :, None], correlations, jnp.zeros_like(correlations))
    weighted = jnp.einsum("aij,ajn->ain", coefs, correlations, precision=lax.Precision.HIGHEST)
    return (correlations, weighted)


def shards(orbitals, projectors, sphere_start, proj_count, owner_slab, correlation_coef):
    band_index = lax.axis_index("band")
    slab = lax.axis_index("grid")
    nbands = lax.axis_size("band")
    total_rows = orbitals.shape[0] * lax.axis_size("grid")
    chosen = slab_atoms(owner_slab, slab)
    weights = projectors[chosen]
    counts = proj_count[chosen]
    coefs = correlation_coef[chosen]
    gathered = lax.all_gather(orbitals, "band", axis=1, tiled=True)
    width = orbitals.shape[1]
    width_all = gathered.shape[1]
    gram_panel = jnp.dot(orbitals.T, gathered, preferred_element_type=jnp.float32) * (
        1.0 / total_rows
    )
    valid = jnp.ones((A_SLAB,), dtype=bool)
    correlations, weighted = atom_terms(
        gathered, weights, sphere_start[chosen], counts, coefs, valid
    )
    panel_weighted = lax.dynamic_slice_in_dim(weighted, band_index * width, width, 2)
    paw = jnp.dot(
        panel_weighted.reshape(-1, width).T,
        correlations.reshape(-1, width_all),
        precision=lax.Precision.HIGHEST,
    )
    panel_total = lax.psum(gram_panel + paw, "grid")
    metric = lax.all_gather(panel_total, "band", axis=0, tiled=True)
    height = orbitals.shape[0] // nbands
    mine = lax.dynamic_slice_in_dim(gathered, band_index * height, height, 0)
    inverse = inverse_factor(metric).astype(jnp.bfloat16)
    return jnp.dot(mine, inverse.T, preferred_element_type=jnp.float32).astype(jnp.bfloat16)


def solution(mesh):
    in_specs = (P("grid", "band"), P(), P(), P(), P(), P())
    out_specs = P(("grid", "band"), None)
    return jax.shard_map(shards, mesh=mesh, in_specs=in_specs, out_specs=out_specs, check_vma=False)
```

profile of v0, /device:TPU:1, one launch (start us, length us, event | category | flops | bytes accessed | tf_op | source)
XLA Modules:
  0.0 1023.8 jit_solution(12298596556159580187)
XLA Ops:
  15.4 50.7 %all-gather.3.cloned.1.call-done = bf16[2048,2048]{1,0:T(8,128)(2,1)} async-done(((bf16[2048,256]{1,0:T(8,128)(2,1)}), bf16[2048,2048]{1,0:T(8,128)(2,1)}) %all-gather.3.cloned.1.call-update) | async-done | bytes 8388624 | tf_op jit(solution)/shard_map/all_gather | solution.py:62
  66.1 25.7 %while.9 = (s32[]{:T(128)}, bf16[2048,2048]{1,0:T(8,128)(2,1)}, s32[8,2]{0,1:T(2,128)S(1)}, bf16[8,128,2048]{2,1,0:T(8,128)(2,1)}, s32[]{:T(128)}) while((s32[]{:T(128)}, bf16[2048,2048]{1,0:T(8,128)(2,1)}, s32[8,2]{0,1:T(2,128)S(1)}, bf16[8,128,2048]{2,1,0:T(8,128)(2,1)}, s32[]{:T(128)}) %tuple.104), condition=%wide.while_cond.1, body=%wide.while_body.1.sunk | while | flops 2 | bytes 1049189 | solution.py:41
  95.3 6.8 convolution_multiply_fusion
  105.5 90.3 %all-reduce.7.cloned.1.call-done = f32[256,2048]{0,1:T(8,128)} async-done(((f32[256,2048]{0,1:T(8,128)}), f32[256,2048]{0,1:T(8,128)}) %all-reduce.7.cloned.1.call-update) | async-done | bytes 2097168 | tf_op jit(solution)/shard_map/psum | solution.py:78
  196.0 87.6 %all-gather.5.cloned.1.call-done = f32[2048,2048]{0,1:T(8,128)} async-done(((f32[256,2048]{0,1:T(8,128)}), f32[2048,2048]{0,1:T(8,128)}) %all-gather.5.cloned.1.call-update) | async-done | bytes 16777232 | tf_op jit(solution)/shard_map/all_gather | solution.py:79
  286.7 11.7 %cholesky.462 = f32[128,128]{1,0:T(8,128)S(1)} custom-call(f32[128,128]{1,0:T(8,128)S(1)} %cholesky.746), custom_call_target="Cholesky" | custom-call | tf_op jit(solution)/shard_map/jit(cholesky)/cholesky | solution.py:14
  298.5 9.8 custom-call.35
  309.0 11.7 %cholesky.481 = f32[128,128]{1,0:T(8,128)S(1)} custom-call(f32[128,128]{1,0:T(8,128)S(1)} %cholesky.750), custom_call_target="Cholesky" | custom-call | tf_op jit(solution)/shard_map/jit(cholesky)/cholesky | solution.py:14
  320.8 10.3 %custom-call.36 = f32[1,128,128]{1,2,0:T(8,128)S(1)} custom-call(f32[1,128,128]{2,1,0:T(8,128)S(1)} %get-tuple-element.131), custom_call_target="InvertDiagBlocksLowerTriangular" | custom-call | tf_op jit(solution)/shard_map/jit(cholesky)/cholesky | solution.py:14
  331.7 11.7 %cholesky.502 = f32[128,128]{1,0:T(8,128)S(1)} custom-call(f32[128,128]{1,0:T(8,128)S(1)} %cholesky.755), custom_call_target="Cholesky" | custom-call | tf_op jit(solution)/shard_map/jit(cholesky)/cholesky | solution.py:14
  343.5 9.8 custom-call.37
  353.9 11.7 %cholesky.519 = f32[128,128]{1,0:T(8,128)S(1)} custom-call(f32[128,128]{1,0:T(8,128)S(1)} %convolution_subtract_fusion.25), custom_call_target="Cholesky" | custom-call | tf_op jit(solution)/shard_map/jit(cholesky)/cholesky | solution.py:14
  370.4 7.6 while.10
  378.1 39.3 %custom-call.38 = f32[4,128,128]{1,2,0:T(8,128)S(1)} custom-call(f32[4,128,128]{2,1,0:T(8,128)S(1)} %get-tuple-element.43), custom_call_target="InvertDiagBlocksLowerTriangular" | custom-call | tf_op jit(solution)/shard_map/triangular_solve/custom-call.3 | solution.py:16
  435.0 12.1 %cholesky.534 = f32[128,128]{1,0:T(8,128)S(1)} custom-call(f32[128,128]{1,0:T(8,128)S(1)} %cholesky.759), custom_call_target="Cholesky" | custom-call | tf_op jit(solution)/shard_map/jit(cholesky)/cholesky | solution.py:14
  447.3 9.8 custom-call.39
  459.6 11.7 %cholesky.553 = f32[128,128]{1,0:T(8,128)S(1)} custom-call(f32[128,128]{1,0:T(8,128)S(1)} %cholesky.763), custom_call_target="Cholesky" | custom-call | tf_op jit(solution)/shard_map/jit(cholesky)/cholesky | solution.py:14
  471.4 9.8 custom-call.40
  482.8 11.9 %cholesky.574 = f32[128,128]{1,0:T(8,128)S(1)} custom-call(f32[128,128]{1,0:T(8,128)S(1)} %cholesky.768), custom_call_target="Cholesky" | custom-call | tf_op jit(solution)/shard_map/jit(cholesky)/cholesky | solution.py:14
  494.7 9.8 custom-call.41
  505.9 11.7 %cholesky.591 = f32[128,128]{1,0:T(8,128)S(1)} custom-call(f32[128,128]{1,0:T(8,128)S(1)} %convolution_subtract_fusion.24), custom_call_target="Cholesky" | custom-call | tf_op jit(solution)/shard_map/jit(cholesky)/cholesky | solution.py:14
  523.8 11.2 %while.11 = (s32[]{:T(128)}, f32[512,512]{1,0:T(8,128)}, s32[4,2]{0,1:T(2,128)S(1)}, f32[4,128,128]{2,1,0:T(8,128)S(1)}, s32[]{:T(128)}) while((s32[]{:T(128)}, f32[512,512]{1,0:T(8,128)}, s32[4,2]{0,1:T(2,128)S(1)}, f32[4,128,128]{2,1,0:T(8,128)S(1)}, s32[]{:T(128)}) %tuple.125), condition=%wide.while_cond.clone, body=%wide.while_body.clone.sunk | while | flops 2 | bytes 131189 | solution.py:16
  535.1 39.5 %custom-call.42 = f32[4,128,128]{1,2,0:T(8,128)S(1)} custom-call(f32[4,128,128]{2,1,0:T(8,128)S(1)} %get-tuple-element.44), custom_call_target="InvertDiagBlocksLowerTriangular" | custom-call | tf_op jit(solution)/shard_map/triangular_solve/custom-call.3 | solution.py:16
  583.3 7.0 fusion.173
  590.2 28.5 %fusion.9 = f32[1024,1024]{1,0:T(8,128)S(1)} fusion(f32[2048,2048]{0,1:T(8,128)} %all-gather.5.cloned.1.call-done, f32[512,512]{1,0:T(8,128)S(1)} %copy-done.5, f32[128,512]{1,0:T(8,128)S(1)} %fusion.125, f32[128,512]{1,0:T(8,128)S(1)} %fusion.126, f32[128,512]{1,0:T(8,128)S(1)} %fusion.128, f32[128,512]{1,0:T(8,128)S(1)} %fusion.81, ...), kind=kOutput, calls=%fused_computation.24 | convolution fusion | flops 12892241920 | bytes 11534336 | tf_op jit(solution)/shard_map/dot_general | solution.py:19
  618.8 18.2 %slice_subtract_fusion = f32[1024,1024]{0,1:T(8,128)} fusion(f32[2048,2048]{0,1:T(8,128)} %all-gather.5.cloned.1.call-done, f32[1024,1024]{1,0:T(8,128)S(1)} %fusion.9), kind=kOutput, calls=%fused_computation.26 | convolution fusion | flops 12885950464 | bytes 16777216 | tf_op jit(solution)/shard_map/dot_general | solution.py:20
  643.3 11.7 %cholesky.606 = f32[128,128]{1,0:T(8,128)S(1)} custom-call(f32[128,128]{1,0:T(8,128)S(1)} %cholesky.772), custom_call_target="Cholesky" | custom-call | tf_op jit(solution)/shard_map/jit(cholesky)/cholesky | solution.py:14
  655.1 9.8 custom-call.43
  667.5 11.7 %cholesky.625 = f32[128,128]{1,0:T(8,128)S(1)} custom-call(f32[128,128]{1,0:T(8,128)S(1)} %cholesky.776), custom_call_target="Cholesky" | custom-call | tf_op jit(solution)/shard_map/jit(cholesky)/cholesky | solution.py:14
  679.2 10.3 %custom-call.44 = f32[1,128,128]{1,2,0:T(8,128)S(1)} custom-call(f32[1,128,128]{2,1,0:T(8,128)S(1)} %get-tuple-element.111), custom_call_target="InvertDiagBlocksLowerTriangular" | custom-call | tf_op jit(solution)/shard_map/jit(cholesky)/cholesky | solution.py:14
  691.1 11.7 %cholesky.646 = f32[128,128]{1,0:T(8,128)S(1)} custom-call(f32[128,128]{1,0:T(8,128)S(1)} %cholesky.781), custom_call_target="Cholesky" | custom-call | tf_op jit(solution)/shard_map/jit(cholesky)/cholesky | solution.py:14
  702.8 9.8 custom-call.45
  714.1 11.7 %cholesky.663 = f32[128,128]{1,0:T(8,128)S(1)} custom-call(f32[128,128]{1,0:T(8,128)S(1)} %convolution_subtract_fusion.23), custom_call_target="Cholesky" | custom-call | tf_op jit(solution)/shard_map/jit(cholesky)/cholesky | solution.py:14
  732.3 11.7 %while.12 = (s32[]{:T(128)}, f32[512,512]{1,0:T(8,128)}, s32[4,2]{0,1:T(2,128)S(1)}, f32[4,128,128]{2,1,0:T(8,128)S(1)}, s32[]{:T(128)}) while((s32[]{:T(128)}, f32[512,512]{1,0:T(8,128)}, s32[4,2]{0,1:T(2,128)S(1)}, f32[4,128,128]{2,1,0:T(8,128)S(1)}, s32[]{:T(128)}) %tuple.126), condition=%wide.while_cond.clone.1, body=%wide.while_body.clone.1.sunk | while | flops 2 | bytes 131189 | solution.py:16
  744.0 39.3 %custom-call.46 = f32[4,128,128]{1,2,0:T(8,128)S(1)} custom-call(f32[4,128,128]{2,1,0:T(8,128)S(1)} %get-tuple-element.45), custom_call_target="InvertDiagBlocksLowerTriangular" | custom-call | tf_op jit(solution)/shard_map/triangular_solve/custom-call.3 | solution.py:16
  801.1 17.2 %fusion.172 = f32[1024,1024]{1,0:T(8,128)} fusion(f32[1024,1024]{1,0:T(8,128)S(1)} %copy-done.17, f32[512,512]{1,0:T(8,128)S(1)} %copy-done.6, f32[128,512]{1,0:T(8,128)S(1)} %copy-done.12, f32[128,512]{1,0:T(8,128)S(1)} %fusion.126, f32[128,512]{1,0:T(8,128)S(1)} %fusion.128, f32[128,512]{1,0:T(8,128)S(1)} %fusion.81, f32[512,512]{1,0:T(8,128)S(1)} %copy-done.3), kind=kOutput, calls=%fused_computation.324 | convolution fusion | flops 12892241920 | bytes 11534336 | tf_op jit(solution)/shard_map/dot_general | solution.py:24
  822.1 11.7 %cholesky.678 = f32[128,128]{1,0:T(8,128)S(1)} custom-call(f32[128,128]{1,0:T(8,128)S(1)} %cholesky.785), custom_call_target="Cholesky" | custom-call | tf_op jit(solution)/shard_map/jit(cholesky)/cholesky | solution.py:14
  833.9 9.8 custom-call.47
  846.3 11.7 %cholesky.697 = f32[128,128]{1,0:T(8,128)S(1)} custom-call(f32[128,128]{1,0:T(8,128)S(1)} %cholesky.789), custom_call_target="Cholesky" | custom-call | tf_op jit(solution)/shard_map/jit(cholesky)/cholesky | solution.py:14
  858.0 10.0 custom-call.48
  869.6 11.7 %cholesky.718 = f32[128,128]{1,0:T(8,128)S(1)} custom-call(f32[128,128]{1,0:T(8,128)S(1)} %cholesky.794), custom_call_target="Cholesky" | custom-call | tf_op jit(solution)/shard_map/jit(cholesky)/cholesky | solution.py:14
  881.3 9.8 custom-call.49
  892.6 11.7 %cholesky.735 = f32[128,128]{1,0:T(8,128)S(1)} custom-call(f32[128,128]{1,0:T(8,128)S(1)} %convolution_subtract_fusion.22), custom_call_target="Cholesky" | custom-call | tf_op jit(solution)/shard_map/jit(cholesky)/cholesky | solution.py:14
  911.1 12.0 %while.13 = (s32[]{:T(128)}, f32[512,512]{1,0:T(8,128)}, s32[4,2]{0,1:T(2,128)S(1)}, f32[4,128,128]{2,1,0:T(8,128)S(1)}, s32[]{:T(128)}) while((s32[]{:T(128)}, f32[512,512]{1,0:T(8,128)}, s32[4,2]{0,1:T(2,128)S(1)}, f32[4,128,128]{2,1,0:T(8,128)S(1)}, s32[]{:T(128)}) %tuple.127), condition=%wide.while_cond.clone.2, body=%wide.while_body.clone.2.sunk | while | flops 2 | bytes 131189 | solution.py:16
  923.1 39.3 %custom-call.50 = f32[4,128,128]{1,2,0:T(8,128)S(1)} custom-call(f32[4,128,128]{2,1,0:T(8,128)S(1)} %get-tuple-element.46), custom_call_target="InvertDiagBlocksLowerTriangular" | custom-call | tf_op jit(solution)/shard_map/triangular_solve/custom-call.3 | solution.py:16
  970.3 6.0 fusion.16
  976.3 13.6 %negate_convert_fusion = bf16[1024,1024]{1,0:T(8,128)(2,1)S(1)} fusion(f32[1024,1024]{1,0:T(8,128)S(1)} %copy-done.18, f32[512,512]{1,0:T(8,128)S(1)} %copy-done.7, f32[128,512]{1,0:T(8,128)S(1)} %fusion.113, f32[128,512]{1,0:T(8,128)S(1)} %fusion.114, f32[128,512]{1,0:T(8,128)S(1)} %fusion.116, f32[128,512]{1,0:T(8,128)S(1)} %fusion.77, ...), kind=kOutput, calls=%fused_computation.30 | convolution fusion | flops 12894339072 | bytes 9437184 | tf_op jit(solution)/shard_map/dot_general | solution.py:22
  989.9 26.9 %fusion.13 = bf16[256,2048]{1,0:T(8,128)(2,1)} fusion(bf16[1024,1024]{1,0:T(8,128)(2,1)S(1)} %copy-done.13, bf16[1024,1024]{1,0:T(8,128)(2,1)S(1)} %fusion.16, bf16[1024,1024]{1,0:T(8,128)(2,1)S(1)} %negate_convert_fusion, bf16[2048,2048]{1,0:T(8,128)(2,1)} %get-tuple-element.377, s32[]{:T(128)S(6)} %select_n.31), kind=kOutput, calls=%fused_computation.34 | convolution fusion | flops 2181562368 | bytes 8388612 | tf_op jit(solution)/shard_map/dot_general | solution.py:83
  (263 shorter events, 181.6 us)
Async XLA Ops:
  6.5 4.0 copy-start
  6.5 59.5 %all-gather.3.cloned.1.call-start = ((), (), s32[]{:S(2)}) async-start(), calls=%async_computation | async-start | bytes 9437184 | tf_op jit(solution)/shard_map/all_gather | solution.py:62
  7.3 188.6 %all-reduce.7.cloned.1.call-start = ((), (), s32[]{:S(2)}) async-start(), calls=%async_computation.1 | async-start | bytes 4194304 | tf_op jit(solution)/shard_map/psum | solution.py:78
  91.7 3.5 copy-start.14
  105.3 178.3 %all-gather.5.cloned.1.call-start = ((), (), s32[]{:S(2)}) async-start(), calls=%async_computation.2 | async-start | bytes 18874368 | tf_op jit(solution)/shard_map/all_gather | solution.py:79
  434.0 1.0 copy-start.8
  574.6 3.5 copy-start.15
  575.0 8.2 copy-start.5
  581.4 8.8 copy-start.11
  583.3 35.5 %copy-start.2 = (f32[512,512]{1,0:T(8,128)}, f32[512,512]{1,0:T(8,128)S(1)}, u32[]{:S(2)}) copy-start(f32[512,512]{1,0:T(8,128)S(1)} %convolution_negate_fusion.1) | copy-start | bytes 3145732
  618.8 18.2 %copy-start.16 = (f32[1024,1024]{1,0:T(8,128)}, f32[1024,1024]{1,0:T(8,128)S(1)}, u32[]{:S(2)}) copy-start(f32[1024,1024]{1,0:T(8,128)S(1)} %fusion.9) | copy-start | bytes 12582916
  642.3 1.0 copy-start.10
  793.9 7.3 copy-start.3
  793.9 7.3 copy-start.6
  793.9 7.2 copy-start.12
  793.9 7.2 copy-start.17
  821.1 1.0 copy-start.9
  909.8 58.6 %copy-start.4 = (f32[512,512]{1,0:T(8,128)S(1)}, f32[512,512]{1,0:T(8,128)}, u32[]{:S(2)}) copy-start(f32[512,512]{1,0:T(8,128)} %fusion.170) | copy-start | bytes 3145732
  962.9 7.4 copy-start.7
  968.4 7.9 copy-start.18
  976.2 13.7 %copy-start.13 = (bf16[1024,1024]{1,0:T(8,128)(2,1)S(1)}, bf16[1024,1024]{1,0:T(8,128)(2,1)}, u32[]{:S(2)}) copy-start(bf16[1024,1024]{1,0:T(8,128)(2,1)} %fusion.173) | copy-start | bytes 6291460
  989.9 26.9 %copy-start.1 = (bf16[128,8,128]{2,1,0:T(8,128)(2,1)S(1)}, bf16[128,8,128]{2,1,0:T(8,128)(2,1)}, u32[]{:S(2)}) copy-start(bf16[128,8,128]{2,1,0:T(8,128)(2,1)} %param.10) | copy-start | bytes 786436
Sparse Core Ops, SparseCore 0:
  9.0 57.0 all-gather.2
  105.4 90.3 all-reduce.6
  197.5 86.0 all-gather.4
where the time goes:
time: 1030 us; the launch traced here: 1020 us
  other arithmetic  503 us (49%)
  waiting for transfers between devices  229 us (22%)
  matrix products  182 us (18%)
  local copies, waits for them, and re-layouts  84.3 us (8%)
  between operations  25.2 us (2%)
    another operation x59, other arithmetic, inverse_factor(): lower = jnp.linalg.cholesky(matrix)  317 us
    another operation x11, other arithmetic, inverse_factor(): lax.linalg.triangular_solve(lower, identity, left_side=True, lower=True)  163 us
    psum x1, waiting for transfers between devices, shards(): panel_total = lax.psum(gram_panel + paw, 'grid')  90.3 us
    all_gather x1, waiting for transfers between devices, shards(): metric = lax.all_gather(panel_total, 'band', axis=0, tiled=True)  87.6 us
    all_gather x1, waiting for transfers between devices, shards(): gathered = lax.all_gather(orbitals, 'band', axis=1, tiled=True)  50.7 us
    another operation x53, local copies, waits for them, and re-layouts, inverse_factor(): lax.linalg.triangular_solve(lower, identity, left_side=True, lower=True)  42.3 us
    dot_general x3, matrix products, inverse_factor(): jnp.dot(matrix[half:, :half], upper_inv.T, precision=lax.Precision.HIGHEST)  38 us
    dot_general x1, matrix products, shards(): jnp.dot(mine, inverse.T, preferred_element_type=jnp.float32)  26.9 us
  transfers between devices with their start and end apart: 3, of which 3 were waited for; matrix products, arithmetic and copies ran while one was open for 1% of the time, Pallas kernels for 0%

commit v1 on v0

--- a/solution.py
+++ b/solution.py
@@ -1,32 +1,113 @@
 import jax
 import jax.numpy as jnp
 from jax import lax
+from jax.experimental import pallas as pl
+from jax.experimental.pallas import tpu as pltpu
 from jax.sharding import PartitionSpec as P
 
+F32 = jnp.float32
+BF = jnp.bfloat16
 SPH = 128
 NPMAX = 8
 A_SLAB = 8
 
 
-def inverse_factor(matrix):
-    order = matrix.shape[0]
-    if order <= 512 or order % 2 != 0:
-        lower = jnp.linalg.cholesky(matrix)
-        identity = jnp.eye(order, dtype=matrix.dtype)
-        return lax.linalg.triangular_solve(lower, identity, left_side=True, lower=True)
-    half = order // 2
-    upper_inv = inverse_factor(matrix[:half, :half])
-    below = jnp.dot(matrix[half:, :half], upper_inv.T, precision=lax.Precision.HIGHEST)
-    schur = matrix[half:, half:] - jnp.dot(below, below.T, precision=lax.Precision.HIGHEST)
-    lower_inv = inverse_factor(schur)
-    corner = -jnp.dot(
-        lower_inv,
-        jnp.dot(below, upper_inv, precision=lax.Precision.HIGHEST),
-        precision=lax.Precision.HIGHEST,
-    )
-    top = jnp.concatenate([upper_inv, jnp.zeros((half, order - half), matrix.dtype)], axis=1)
-    bottom = jnp.concatenate([corner, lower_inv], axis=1)
-    return jnp.concatenate([top, bottom], axis=0)
+def chol_inv_128(a_ref, w_ref):
+    n=128; T=16
+    A=[a_ref[8*t:8*t+8,:] for t in range(T)]
+    lane=lax.broadcasted_iota(jnp.int32,(8,128),1)
+    sub=lax.broadcasted_iota(jnp.int32,(8,128),0)
+    W=[jnp.where(lane==sub+8*t,1.0,0.0).astype(F32) for t in range(T)]
+    for g in range(T):
+        C=[[jnp.broadcast_to(A[t][:,8*g+c:8*g+c+1],(8,128)) for t in range(T)] if True else None for c in range(0)]
+        C=[{t:jnp.broadcast_to(A[t][:,8*g+c:8*g+c+1],(8,128)) for t in range(g,T)} for c in range(8)]
+        S=jnp.ones((8,128),F32)
+        for c in range(8):
+            d=jnp.broadcast_to(C[c][g][c:c+1,:],(8,128))
+            S=jnp.where(sub==c,d,S)
+            inv=1.0/d
+            Cc=dict(C[c])
+            if c<7:
+                Cc[g]=jnp.where(sub>c,C[c][g],0.0)
+            ra=jnp.broadcast_to(A[g][c:c+1,:],(8,128))*inv
+            rw=jnp.broadcast_to(W[g][c:c+1,:],(8,128))*inv
+            rc={j:jnp.broadcast_to(C[j][g][c:c+1,:],(8,128))*inv for j in range(c+1,8)}
+            t0=g if c<7 else g+1
+            for t in range(t0,T):
+                for j in range(c+1,8):
+                    C[j][t]=C[j][t]-Cc[t]*rc[j]
+                A[t]=A[t]-Cc[t]*ra
+                W[t]=W[t]-Cc[t]*rw
+        w_ref[8*g:8*g+8,:]=W[g]*lax.rsqrt(S)
+
+
+B=256
+HI=lax.Precision.HIGHEST
+def splt(x):
+    h=x.astype(BF); return h,(x-h.astype(F32)).astype(BF)
+def nt(a,b,prec=None):
+    return lax.dot_general(a,b,(((1,),(1,)),((),())),preferred_element_type=F32,precision=prec)
+def tn(a,b,prec=None):
+    return lax.dot_general(a,b,(((0,),(0,)),((),())),preferred_element_type=F32,precision=prec)
+def nn(a,b,prec=None):
+    return lax.dot_general(a,b,(((1,),(0,)),((),())),preferred_element_type=F32,precision=prec)
+
+def fac_kernel(m_ref, x_ref, o_ref, T, UT, U, Wd, Ws, Wt, sem):
+    NBK=8
+    cps=[]
+    for i in range(NBK):
+        for c in range(i,NBK):
+            cp=pltpu.make_async_copy(m_ref.at[pl.ds(B*i,B),pl.ds(B*c,B)],T.at[i,c],sem.at[i])
+            cp.start(); cps.append((i,cp))
+    for c in range(NBK):
+        T[8,c]=x_ref[:,B*c:B*c+B].astype(F32)
+    for i,cp in cps: cp.wait()
+    Wd[...]=jnp.zeros((B,B),F32)
+    def step(j,_):
+        D=T.at[j,j]
+        chol_inv_128(D.at[pl.ds(0,128),pl.ds(0,128)],Wd.at[pl.ds(0,128),pl.ds(0,128)])
+        W1=Wd[0:128,0:128]
+        u12=nn(W1,T[j,j,0:128,128:256],HI)
+        T[j,j,128:256,128:256]=T[j,j,128:256,128:256]-tn(u12,u12,HI)
+        chol_inv_128(D.at[pl.ds(128,128),pl.ds(128,128)],Wd.at[pl.ds(128,128),pl.ds(128,128)])
+        W2=Wd[128:256,128:256]
+        Wd[128:256,0:128]=-nn(W2,tn(u12,W1,HI),HI)
+        h,l=splt(Wd[...])
+        Ws[:,0:B]=h; Ws[:,B:2*B]=h; Ws[:,2*B:3*B]=l
+        Wt[:,0:B]=h; Wt[:,B:2*B]=l; Wt[:,2*B:3*B]=h
+        h,l=splt(T[8,j])
+        r=nt(jnp.concatenate([h,h,l],axis=1),Wt[...])
+        h=r.astype(BF)
+        o_ref[j]=h
+        l=(r-h.astype(F32)).astype(BF)
+        UT[8,:,0:B]=h; UT[8,:,B:2*B]=h; UT[8,:,2*B:3*B]=l
+        def pan(c,_):
+            h,l=splt(T[j,c])
+            u=nn(Ws[...],jnp.concatenate([h,l,h],axis=0))
+            h,l=splt(u)
+            U[c,0:B,:]=h; U[c,B:2*B,:]=l; U[c,2*B:3*B,:]=h
+            h,l=splt(u.T)
+            UT[c,:,0:B]=h; UT[c,:,B:2*B]=h; UT[c,:,2*B:3*B]=l
+            return 0
+        lax.fori_loop(j+1,NBK,pan,0)
+        def row(i,_):
+            def col(c,_):
+                T[i,c]=T[i,c]-nn(UT[i],U[c])
+                return 0
+            lax.fori_loop(jnp.where(i==8,j+1,i),NBK,col,0)
+            return 0
+        lax.fori_loop(j+1,NBK+1,row,0)
+        return 0
+    lax.fori_loop(0,NBK,step,0)
+
+def factor_rotate(metric, mine):
+    o=pl.pallas_call(fac_kernel,out_shape=jax.ShapeDtypeStruct((8,B,B),BF),
+      in_specs=[pl.BlockSpec(memory_space=pltpu.HBM),pl.BlockSpec(memory_space=pltpu.VMEM)],
+      out_specs=pl.BlockSpec(memory_space=pltpu.VMEM),
+      scratch_shapes=[pltpu.VMEM((9,8,B,B),F32),pltpu.VMEM((9,B,3*B),BF),pltpu.VMEM((8,3*B,B),BF),
+         pltpu.VMEM((B,B),F32),pltpu.VMEM((B,3*B),BF),pltpu.VMEM((B,3*B),BF),pltpu.SemaphoreType.DMA((8,))],
+      compiler_params=pltpu.CompilerParams(vmem_limit_bytes=56*2**20))(metric,mine)
+    return o.transpose(1,0,2).reshape(B,8*B)
 
 
 def slab_atoms(owner_slab, slab):
@@ -79,8 +160,7 @@
     metric = lax.all_gather(panel_total, "band", axis=0, tiled=True)
     height = orbitals.shape[0] // nbands
     mine = lax.dynamic_slice_in_dim(gathered, band_index * height, height, 0)
-    inverse = inverse_factor(metric).astype(jnp.bfloat16)
-    return jnp.dot(mine, inverse.T, preferred_element_type=jnp.float32).astype(jnp.bfloat16)
+    return factor_rotate(metric, mine)
 
 
 def solution(mesh):

time: 1030 us -> 408 us (0.40)
  other arithmetic: 503 us -> 3.29 us
  matrix products: 182 us -> 9.1 us
  Pallas kernels: 0 us -> 118 us
  local copies, waits for them, and re-layouts: 84.3 us -> 35.7 us
  between operations: 25.2 us -> 13.2 us
    another operation x72 -> x0, other arithmetic: 493 us -> none  [the longest x59 317 us: inverse_factor(): lower = jnp.linalg.cholesky(matrix)]
    dot_general x13 -> x0, matrix products: 129 us -> none  [the longest x3 38 us: inverse_factor(): jnp.dot(matrix[half:, :half], upper_inv.T, precision=lax.Precision.HIGHEST)]
    pallas_call x0 -> x1, Pallas kernels: none -> 118 us  [factor_rotate(): pl.pallas_call(fac_kernel, out_shape=jax.ShapeDtypeStruct((8, B, B), BF),...]
    another operation x69 -> x0, local copies, waits for them, and re-layouts: 42.9 us -> none  [the longest x53 42.3 us: inverse_factor(): lax.linalg.triangular_solve(lower, identity, left_side=True, lower=True)]
    another operation x52 -> x0, matrix products: 39.7 us -> none  [the longest x28 21.4 us: inverse_factor(): lax.linalg.triangular_solve(lower, identity, left_side=True, lower=True)]
  transfers between devices with their start and end apart: 3 -> 3, of which waited for: 3 -> 3; matrix products, arithmetic and copies ran while one was open for 1% -> 3% of each run, Pallas kernels for 0% -> 0%
where the time goes in v1:
time: 408 us; the launch traced here: 407 us
  waiting for transfers between devices  227 us (56%)
  Pallas kernels  118 us (29%)
  local copies, waits for them, and re-layouts  35.7 us (9%)
  between operations  13.2 us (3%)
  matrix products  9.1 us (2%)
    pallas_call x1, Pallas kernels, factor_rotate(): pl.pallas_call(fac_kernel, out_shape=jax.ShapeDtypeStruct((8, B, B), BF),...  118 us
    psum x1, waiting for transfers between devices, shards(): panel_total = lax.psum(gram_panel + paw, 'grid')  90.4 us
    all_gather x1, waiting for transfers between devices, shards(): metric = lax.all_gather(panel_total, 'band', axis=0, tiled=True)  85.4 us
    all_gather x1, waiting for transfers between devices, shards(): gathered = lax.all_gather(orbitals, 'band', axis=1, tiled=True)  50.7 us
    gather x24, local copies, waits for them, and re-layouts  25.8 us
  transfers between devices with their start and end apart: 3, of which 3 were waited for; matrix products, arithmetic and copies ran while one was open for 3% of the time, Pallas kernels for 0%

profile of v1, /device:TPU:1, one launch (start us, length us, event | category | flops | bytes accessed | tf_op | source)
XLA Modules:
  0.0 407.3 jit_solution(16448288216030789313)
XLA Ops:
  6.5 0.7 all-gather.3.cloned.1.call-update
  7.3 0.0 all-reduce.3.cloned.1.call-start
  7.3 0.7 fusion.3
  8.0 2.5 sort.17
  10.5 1.3 gather_fusion.3
  11.9 1.3 gather_fusion.1
  13.2 0.6 gather_fusion.2
  13.7 1.0 copy.7
  14.7 0.6 gather_fusion
  15.3 0.1 iota_compare_fusion
  15.4 50.7 %all-gather.3.cloned.1.call-done = bf16[2048,2048]{1,0:T(8,128)(2,1)} async-done(((bf16[2048,256]{1,0:T(8,128)(2,1)}), bf16[2048,2048]{1,0:T(8,128)(2,1)}) %all-gather.3.cloned.1.call-update) | async-done | bytes 8388624 | tf_op jit(solution)/shard_map/all_gather | solution.py:143
  66.1 25.8 %while.1 = (s32[]{:T(128)}, bf16[2048,2048]{1,0:T(8,128)(2,1)}, s32[8,2]{0,1:T(2,128)S(1)}, bf16[8,128,2048]{2,1,0:T(8,128)(2,1)}, s32[]{:T(128)}) while((s32[]{:T(128)}, bf16[2048,2048]{1,0:T(8,128)(2,1)}, s32[8,2]{0,1:T(2,128)S(1)}, bf16[8,128,2048]{2,1,0:T(8,128)(2,1)}, s32[]{:T(128)}) %tuple.16), condition=%wide.while_cond, body=%wide.while_body.sunk | while | flops 2 | bytes 1049189 | solution.py:122
  66.1 0.1 constant_dynamic-slice_fusion.3
  66.1 0.5 slice.25
  66.6 2.6 bitcast_dynamic-update-slice_fusion.2
  69.3 0.1 constant_dynamic-slice_fusion.3
  69.4 0.5 slice.25
  69.9 2.6 bitcast_dynamic-update-slice_fusion.2
  72.5 0.1 constant_dynamic-slice_fusion.3
  72.6 0.5 slice.25
  73.1 2.6 bitcast_dynamic-update-slice_fusion.2
  75.7 0.1 constant_dynamic-slice_fusion.3
  75.8 0.5 slice.25
  76.3 2.6 bitcast_dynamic-update-slice_fusion.2
  79.0 0.1 constant_dynamic-slice_fusion.3
  79.0 0.5 slice.25
  79.5 2.6 bitcast_dynamic-update-slice_fusion.2
  82.2 0.1 constant_dynamic-slice_fusion.3
  82.2 0.5 slice.25
  82.8 2.6 bitcast_dynamic-update-slice_fusion.2
  85.4 0.1 constant_dynamic-slice_fusion.3
  85.5 0.5 slice.25
  86.0 2.6 bitcast_dynamic-update-slice_fusion.2
  88.6 0.1 constant_dynamic-slice_fusion.3
  88.7 0.5 slice.25
  89.2 2.6 bitcast_dynamic-update-slice_fusion.2
  91.8 3.0 convolution_select_fusion
  94.8 0.6 fusion.5
  95.4 1.9 convolution_bitcast_fusion
  97.3 3.7 fusion
  101.0 0.0 all-reduce.3.cloned.1.call-update
  101.0 0.2 all-gather.5.cloned.1.call-start
  101.2 90.4 %all-reduce.3.cloned.1.call-done = f32[256,2048]{1,0:T(8,128)} async-done(((f32[256,2048]{1,0:T(8,128)}), f32[256,2048]{1,0:T(8,128)}) %all-reduce.3.cloned.1.call-update) | async-done | bytes 2097168 | tf_op jit(solution)/shard_map/psum | solution.py:159
  191.6 2.3 constant_dynamic-slice_fusion.1.x_ref
  194.0 85.4 %all-gather.5.cloned.1.call-done.m_ref = f32[2048,2048]{1,0:T(8,128)} async-done(((f32[256,2048]{1,0:T(8,128)}), f32[2048,2048]{1,0:T(8,128)}) %all-gather.5.cloned.1.call-update) | async-done | bytes 16777232 | tf_op jit(solution)/shard_map/all_gather | solution.py:160
  279.4 118.4 %shard_map.64 = bf16[8,256,256]{2,1,0:T(8,128)(2,1)} custom-call(f32[2048,2048]{1,0:T(8,128)} %all-gather.5.cloned.1.call-done.m_ref, bf16[256,2048]{1,0:T(8,128)(2,1)} %constant_dynamic-slice_fusion.1.x_ref), custom_call_target="tpu_custom_call" | custom-call | tf_op jit(solution)/shard_map/pallas_call | solution.py:104
  397.8 1.5 copy.8
  399.3 1.4 copy.9
  (14 shorter events, 0.1 us)
Async XLA Ops:
  6.5 6.6 %copy-start = (bf16[128,8,128]{2,1,0:T(8,128)(2,1)S(1)}, bf16[128,8,128]{2,1,0:T(8,128)(2,1)}, u32[]{:S(2)}) copy-start(bf16[128,8,128]{2,1,0:T(8,128)(2,1)} %param.7) | copy-start | bytes 786436
  6.5 59.5 %all-gather.3.cloned.1.call-start = ((), (), s32[]{:S(2)}) async-start(), calls=%async_computation | async-start | bytes 9437184 | tf_op jit(solution)/shard_map/all_gather | solution.py:143
  7.3 184.4 %all-reduce.3.cloned.1.call-start = ((), (), s32[]{:S(2)}) async-start(), calls=%async_computation.1 | async-start | bytes 4194304 | tf_op jit(solution)/shard_map/psum | solution.py:159
  91.8 5.4 %copy-start.1 = (bf16[2048,2048]{1,0:T(8,128)(2,1)S(1)}, bf16[2048,2048]{1,0:T(8,128)(2,1)}, u32[]{:S(2)}) copy-start(bf16[2048,2048]{1,0:T(8,128)(2,1)} %get-tuple-element.67) | copy-start | bytes 25165828
  94.8 2.5 copy-start.2
  101.0 178.4 %all-gather.5.cloned.1.call-start = ((), (), s32[]{:S(2)}) async-start(), calls=%async_computation.2 | async-start | bytes 18874368 | tf_op jit(solution)/shard_map/all_gather | solution.py:160
Sparse Core Ops, SparseCore 0:
  9.0 57.0 all-gather.2
  101.1 90.4 all-reduce.2
  193.3 86.0 all-gather.4

commit v2 on v1

--- a/solution.py
+++ b/solution.py
@@ -57,11 +57,14 @@
     cps=[]
     for i in range(NBK):
         for c in range(i,NBK):
-            cp=pltpu.make_async_copy(m_ref.at[pl.ds(B*i,B),pl.ds(B*c,B)],T.at[i,c],sem.at[i])
-            cp.start(); cps.append((i,cp))
+            t=PAIRS.index((i,c))
+            for h in range(2):
+                k=len(cps)
+                cp=pltpu.make_async_copy(m_ref.at[t//18,pl.ds((t%18)*512+256*h,256),:],T.at[i,c,:,pl.ds(128*h,128)],sem.at[k])
+                cp.start(); cps.append(cp)
     for c in range(NBK):
-        T[8,c]=x_ref[:,B*c:B*c+B].astype(F32)
-    for i,cp in cps: cp.wait()
+        T[8,c]=x_ref[c].astype(F32)
+    for cp in cps: cp.wait()
     Wd[...]=jnp.zeros((B,B),F32)
     def step(j,_):
         D=T.at[j,j]
@@ -105,61 +108,252 @@
       in_specs=[pl.BlockSpec(memory_space=pltpu.HBM),pl.BlockSpec(memory_space=pltpu.VMEM)],
       out_specs=pl.BlockSpec(memory_space=pltpu.VMEM),
       scratch_shapes=[pltpu.VMEM((9,8,B,B),F32),pltpu.VMEM((9,B,3*B),BF),pltpu.VMEM((8,3*B,B),BF),
-         pltpu.VMEM((B,B),F32),pltpu.VMEM((B,3*B),BF),pltpu.VMEM((B,3*B),BF),pltpu.SemaphoreType.DMA((8,))],
+         pltpu.VMEM((B,B),F32),pltpu.VMEM((B,3*B),BF),pltpu.VMEM((B,3*B),BF),pltpu.SemaphoreType.DMA((72,))],
       compiler_params=pltpu.CompilerParams(vmem_limit_bytes=56*2**20))(metric,mine)
     return o.transpose(1,0,2).reshape(B,8*B)
 
 
-def slab_atoms(owner_slab, slab):
+MESH = pl.DeviceIdType.MESH
+XDT = F32
+
+
+def barrier(peers):
+    sem = pltpu.get_barrier_semaphore()
+    for peer in peers:
+        pl.semaphore_signal(sem, inc=1, device_id=peer, device_id_type=MESH)
+    pl.semaphore_wait(sem, len(peers))
+
+
+def swap_kernel(x_ref, o_ref, ssem, rsem, fsem, gsem):
+    me = lax.axis_index("band")
+    core = lax.rem(me, 2)
+    mate = me + 1 - 2 * core
+    barrier([{"band": lax.rem(me + d, 8)} for d in range(1, 8)])
+    sends = []
+    for d in (4, 3, 5, 2, 6, 1, 7):
+        peer = lax.rem(me + d, 8)
+        cp = pltpu.make_async_remote_copy(
+            src_ref=x_ref.at[pl.ds(pl.multiple_of(256 * peer, 256), 256), :],
+            dst_ref=o_ref.at[lax.rem(peer, 2), me],
+            send_sem=ssem.at[d - 1], recv_sem=rsem.at[d - 1],
+            device_id={"band": peer}, device_id_type=MESH)
+        cp.start()
+        sends.append(cp)
+    own = x_ref.at[pl.ds(pl.multiple_of(256 * me, 256), 256), :]
+    cp0 = pltpu.make_async_remote_copy(
+        src_ref=own, dst_ref=o_ref.at[core, me], send_sem=fsem.at[7], recv_sem=gsem.at[7],
+        device_id={"band": mate}, device_id_type=MESH)
+    cp0.start()
+    lsem = ssem.at[7]
+    loc = pltpu.make_async_copy(own, o_ref.at[core, me], lsem)
+    loc.start()
+    fwd = [cp0]
+    for d, s in zip((1, 7, 2, 6, 3, 5, 4), (5, 6, 3, 4, 1, 2, 0)):
+        sends[s].wait_recv()
+        k = lax.rem(me + 8 - d, 8)
+        cp = pltpu.make_async_remote_copy(
+            src_ref=o_ref.at[core, k], dst_ref=o_ref.at[core, k],
+            send_sem=fsem.at[d - 1], recv_sem=gsem.at[d - 1],
+            device_id={"band": mate}, device_id_type=MESH)
+        cp.start()
+        fwd.append(cp)
+    loc.wait()
+    for cp in fwd:
+        cp.wait()
+    for cp in sends:
+        cp.wait_send()
+
+
+def swap(x):
+    return pl.pallas_call(
+        swap_kernel, out_shape=jax.ShapeDtypeStruct((2, 8, 256, 256), BF),
+        in_specs=[pl.BlockSpec(memory_space=pltpu.VMEM)],
+        out_specs=pl.BlockSpec(memory_space=pltpu.VMEM),
+        scratch_shapes=[pltpu.SemaphoreType.DMA((8,))] * 4,
+        compiler_params=pltpu.CompilerParams(collective_id=0, has_side_effects=True))(x)
+
+
+def gram_kernel(p_tab, q_tab, x_ref, pm_ref, cb_ref, o_ref, L, R):
+    scale = 1.0 / 32768
+    for k in range(8):
+        corr = nn(pm_ref[0], x_ref[0, k]) + nn(pm_ref[1], x_ref[1, k])
+        wgt = nn(cb_ref[...], corr, HI)
+        ch, cl = splt(corr)
+        wh, wl = splt(wgt)
+        R[k, 0:256, :] = x_ref[0, k]
+        R[k, 256:512, :] = x_ref[1, k]
+        R[k, 512:576, :] = ch
+        R[k, 576:640, :] = cl
+        R[k, 640:704, :] = ch
+        lt = jnp.concatenate([x_ref[0, k].astype(F32) * scale, x_ref[1, k].astype(F32) * scale,
+                              wh.astype(F32), wh.astype(F32), wl.astype(F32)], axis=0)
+        L[k] = lt.T.astype(BF)
+
+    def block(t, _):
+        g = nn(L[p_tab[t]], R[q_tab[t]]).astype(XDT)
+        at = pl.multiple_of(t * 512, 512)
+        o_ref[pl.ds(at, 256), :] = g[:, 0:128]
+        o_ref[pl.ds(at + 256, 256), :] = g[:, 128:256]
+        return 0
+    lax.fori_loop(0, 18, block, 0)
+
+
+def gram(p_tab, q_tab, x, pm, cb):
+    vm = pl.BlockSpec(memory_space=pltpu.VMEM)
+    sm = pl.BlockSpec(memory_space=pltpu.SMEM)
+    return pl.pallas_call(
+        gram_kernel, out_shape=jax.ShapeDtypeStruct((9216, 128), XDT),
+        in_specs=[sm, sm, vm, vm, vm], out_specs=vm,
+        scratch_shapes=[pltpu.VMEM((8, 256, 704), BF), pltpu.VMEM((8, 704, 256), BF)],
+        compiler_params=pltpu.CompilerParams(vmem_limit_bytes=40 * 2**20))(p_tab, q_tab, x, pm, cb)
+
+
+def sum_kernel(p_ref, o_ref, r1, r2, r3, s1, s2, ssem, rsem, fsem, gsem):
+    band, grid = lax.axis_index("band"), lax.axis_index("grid")
+    x, core = lax.div(band, 2), lax.rem(band, 2)
+    z, y = lax.div(grid, 4), lax.rem(grid, 4)
+    at = {"x": x, "y": y, "z": z}
+
+    def peer(axis, d):
+        to = lax.rem(at[axis] + d, 4)
+        return {"x": {"band": 2 * to + core}, "y": {"grid": 4 * z + to}, "z": {"grid": 4 * to + y}}[axis]
+
+    orders = ("xyz", "yzx", "zxy")
+    mate = {"band": band + 1 - 2 * core}
+    barrier([peer(a, d) for a in "xyz" for d in (1, 2, 3)] + [mate])
+
+    def rows(start, n):
+        return pl.ds(pl.multiple_of(start, 16), n)
+
+    pend = []
+
+    def send(stage, k, d, src, dst):
+        i = (stage * 3 + k) * 3 + d - 1
+        cp = pltpu.make_async_remote_copy(
+            src_ref=src, dst_ref=dst, send_sem=ssem.at[i], recv_sem=rsem.at[i],
+            device_id=peer(orders[k][stage if stage < 3 else 5 - stage], d), device_id_type=MESH)
+        cp.start()
+        pend.append(cp)
+        return cp
+
+    live = {}
+    for d in (2, 1, 3):
+        for k in range(3):
+            a = lax.rem(at[orders[k][0]] + d, 4)
+            live[k, d] = send(0, k, d, p_ref.at[rows(k * 3072 + a * 768, 768), :], r1.at[k, d - 1])
+    for k in range(3):
+        for d in (1, 3, 2):
+            live[k, d].wait_recv()
+        a = at[orders[k][0]]
+        tot = p_ref[rows(k * 3072 + a * 768, 768), :].astype(F32)
+        for d in range(3):
+            tot = tot + r1[k, d].astype(F32)
+        s1[k] = tot.astype(XDT)
+        for d in (2, 1, 3):
+            b = lax.rem(at[orders[k][1]] + d, 4)
+            live[k, d] = send(1, k, d, s1.at[k, rows(b * 192, 192), :], r2.at[k, d - 1])
+    for k in range(3):
+        for d in (1, 3, 2):
+            live[k, d].wait_recv()
+        b = at[orders[k][1]]
+        tot = s1[k, rows(b * 192, 192), :].astype(F32)
+        for d in range(3):
+            tot = tot + r2[k, d].astype(F32)
+        s2[k] = tot.astype(XDT)
+        for d in (2, 1, 3):
+            c = lax.rem(at[orders[k][2]] + d, 4)
+            live[k, d] = send(2, k, d, s2.at[k, rows(c * 48, 48), :], r3.at[k, d - 1])
+    base = {}
+    for k in range(3):
+        for d in (1, 3, 2):
+            live[k, d].wait_recv()
+        a, b, c = (at[v] for v in orders[k])
+        tot = s2[k, rows(c * 48, 48), :].astype(F32)
+        for d in range(3):
+            tot = tot + r3[k, d].astype(F32)
+        base[k] = (k * 3072 + a * 768, b * 192, c * 48)
+        here = o_ref.at[core, rows(sum(base[k]), 48), :]
+        o_ref[core, rows(sum(base[k]), 48), :] = tot.astype(XDT)
+        for d in (2, 1, 3):
+            live[k, d] = send(3, k, d, here, here)
+    for k in range(3):
+        for d in (1, 3, 2):
+            live[k, d].wait_recv()
+        here = o_ref.at[core, rows(base[k][0] + base[k][1], 192), :]
+        for d in (2, 1, 3):
+            live[k, d] = send(4, k, d, here, here)
+    fwd = []
+
+    def forward(k, d, a):
+        blk = o_ref.at[core, rows(k * 3072 + a * 768, 768), :]
+        cp = pltpu.make_async_remote_copy(
+            src_ref=blk, dst_ref=blk, send_sem=fsem.at[k * 4 + d], recv_sem=gsem.at[k * 4 + d],
+            device_id=mate, device_id_type=MESH)
+        cp.start()
+        fwd.append(cp)
+
+    for k in range(3):
+        for d in (1, 3, 2):
+            live[k, d].wait_recv()
+        here = o_ref.at[core, rows(base[k][0], 768), :]
+        for d in (2, 1, 3):
+            live[k, d] = send(5, k, d, here, here)
+        forward(k, 0, at[orders[k][0]])
+    for d in (1, 3, 2):
+        for k in range(3):
+            live[k, d].wait_recv()
+            forward(k, d, lax.rem(at[orders[k][0]] + 4 - d, 4))
+    for cp in fwd:
+        cp.wait()
+    for cp in pend:
+        cp.wait_send()
+
+
+def total(part):
+    vm = pl.BlockSpec(memory_space=pltpu.VMEM)
+    return pl.pallas_call(
+        sum_kernel, out_shape=jax.ShapeDtypeStruct((2, 9216, 128), XDT),
+        in_specs=[vm], out_specs=vm,
+        scratch_shapes=[pltpu.VMEM((3, 3, 768, 128), XDT), pltpu.VMEM((3, 3, 192, 128), XDT),
+                        pltpu.VMEM((3, 3, 48, 128), XDT), pltpu.VMEM((3, 768, 128), XDT),
+                        pltpu.VMEM((3, 192, 128), XDT),
+                        pltpu.SemaphoreType.DMA((54,)), pltpu.SemaphoreType.DMA((54,)),
+                        pltpu.SemaphoreType.DMA((12,)), pltpu.SemaphoreType.DMA((12,))],
+        compiler_params=pltpu.CompilerParams(collective_id=1, has_side_effects=True,
+                                             vmem_limit_bytes=40 * 2**20))(part)
+
+
+PAIRS = [(i, c) for i in range(8) for c in range(i, 8)]
+
+
+def shards(orbitals, projectors, sphere_start, proj_count, owner_slab, correlation_coef):
+    band = lax.axis_index("band")
+    slab = lax.axis_index("grid")
+    chip, core = band // 2, band % 2
     atoms = owner_slab.shape[0]
-    keyed = jnp.where(owner_slab == slab, 0, 1) * atoms + jnp.arange(atoms, dtype=jnp.int32)
-    return jnp.argsort(keyed, stable=True)[:A_SLAB]
-
-
-def atom_terms(source, weights, starts, counts, coefs, valid):
-
-    def take_rows(offset):
-        return lax.dynamic_slice_in_dim(source, offset, SPH, 0)
-
-    sphere_rows = jax.vmap(take_rows)(starts)
-    correlations = jnp.einsum(
-        "aij,ajn->ain", weights, sphere_rows, preferred_element_type=jnp.float32
-    )
-    active = (jnp.arange(NPMAX)[None, :] < counts[:, None]) & valid[:, None]
-    correlations = jnp.where(active[:, :, None], correlations, jnp.zeros_like(correlations))
-    weighted = jnp.einsum("aij,ajn->ain", coefs, correlations, precision=lax.Precision.HIGHEST)
-    return (correlations, weighted)
-
-
-def shards(orbitals, projectors, sphere_start, proj_count, owner_slab, correlation_coef):
-    band_index = lax.axis_index("band")
-    slab = lax.axis_index("grid")
-    nbands = lax.axis_size("band")
-    total_rows = orbitals.shape[0] * lax.axis_size("grid")
-    chosen = slab_atoms(owner_slab, slab)
-    weights = projectors[chosen]
-    counts = proj_count[chosen]
-    coefs = correlation_coef[chosen]
-    gathered = lax.all_gather(orbitals, "band", axis=1, tiled=True)
-    width = orbitals.shape[1]
-    width_all = gathered.shape[1]
-    gram_panel = jnp.dot(orbitals.T, gathered, preferred_element_type=jnp.float32) * (
-        1.0 / total_rows
-    )
-    valid = jnp.ones((A_SLAB,), dtype=bool)
-    correlations, weighted = atom_terms(
-        gathered, weights, sphere_start[chosen], counts, coefs, valid
-    )
-    panel_weighted = lax.dynamic_slice_in_dim(weighted, band_index * width, width, 2)
-    paw = jnp.dot(
-        panel_weighted.reshape(-1, width).T,
-        correlations.reshape(-1, width_all),
-        precision=lax.Precision.HIGHEST,
-    )
-    panel_total = lax.psum(gram_panel + paw, "grid")
-    metric = lax.all_gather(panel_total, "band", axis=0, tiled=True)
-    height = orbitals.shape[0] // nbands
-    mine = lax.dynamic_slice_in_dim(gathered, band_index * height, height, 0)
+    mask = owner_slab == slab
+    ids = jnp.arange(atoms, dtype=jnp.int32)
+    rank = jnp.sum((ids[None, :] < ids[:, None]) & mask[None, :], axis=1, dtype=jnp.int32)
+    pick = mask[None, :] & (rank[None, :] == jnp.arange(A_SLAB, dtype=jnp.int32)[:, None])
+    starts = jnp.sum(jnp.where(pick, sphere_start[None, :], 0), axis=1)
+    counts = jnp.sum(jnp.where(pick, proj_count[None, :], 0), axis=1)
+    weights = jnp.dot(pick.astype(BF), projectors.reshape(atoms, NPMAX * SPH), preferred_element_type=F32)
+    coefs = jnp.dot(pick.astype(F32), correlation_coef.reshape(atoms, NPMAX * NPMAX), precision=HI)
+    active = jnp.arange(NPMAX, dtype=jnp.int32)[None, :] < counts[:, None]
+    weights = jnp.where(active[:, :, None], weights.reshape(A_SLAB, NPMAX, SPH), 0.0).reshape(64, SPH)
+    place = jnp.repeat(starts // SPH - chip * 4, NPMAX)
+    pm = jnp.where(place[None, :, None, None] == jnp.arange(4, dtype=jnp.int32).reshape(2, 1, 2, 1),
+                   weights[None, :, None, :], 0.0).reshape(2, 64, 256).astype(BF)
+    eye = jnp.eye(A_SLAB, dtype=F32)
+    cb = (eye[:, None, :, None] * coefs.reshape(A_SLAB, NPMAX, 1, NPMAX)).reshape(64, 64)
+    p_all = jnp.asarray([p for p, _ in PAIRS], jnp.int32).reshape(2, 18)
+    q_all = jnp.asarray([q for _, q in PAIRS], jnp.int32).reshape(2, 18)
+    p_tab = jnp.where(core == 0, p_all[0], p_all[1])
+    q_tab = jnp.where(core == 0, q_all[0], q_all[1])
+    rows = swap(orbitals)
+    part = gram(p_tab, q_tab, rows, pm, cb)
+    metric = total(part)
+    mine = lax.dynamic_index_in_dim(rows, core, 0, keepdims=False)
     return factor_rotate(metric, mine)
 
 

time: 408 us -> 234 us (0.57)
  waiting for transfers between devices: 227 us -> 0 us
  Pallas kernels: 118 us -> 218 us
  local copies, waits for them, and re-layouts: 35.7 us -> 12.2 us
  between operations: 13.2 us -> 0.16 us
  matrix products: 9.1 us -> 0.48 us
    all_gather x2 -> x0, waiting for transfers between devices: 136 us -> none  [the longest x1 85.4 us: shards(): metric = lax.all_gather(panel_total, 'band', axis=0, tiled=True)]
    pallas_call x0 -> x3, Pallas kernels: none -> 99 us  [the longest x1 69.4 us: total(): pl.pallas_call(sum_kernel, out_shape=jax.ShapeDtypeStruct((2, 9216, 128),...]
    psum x1 -> x0, waiting for transfers between devices: 90.4 us -> none  [shards(): panel_total = lax.psum(gram_panel + paw, 'grid')]
    gather x28 -> x0, local copies, waits for them, and re-layouts: 29.5 us -> none
    dot_general x4 -> x2, matrix products: 9.1 us -> 0.48 us  [the longest x1 0.31 us: shards(): jnp.dot(pick.astype(F32), correlation_coef.reshape(atoms, NPMAX * NPMAX),...]
    unnamed x7 -> x8, local copies, waits for them, and re-layouts: 1.01 us -> 6.21 us
  transfers between devices with their start and end apart: 3 -> 0, of which waited for: 3 -> 0; matrix products, arithmetic and copies ran while one was open for 3% -> 0% of each run, Pallas kernels for 0% -> 0%
where the time goes in v2:
time: 234 us; the launch traced here: 233 us
  Pallas kernels  218 us (93%)
  local copies, waits for them, and re-layouts  12.2 us (5%)
  other arithmetic  2.5 us (1%)
    pallas_call x1, Pallas kernels, factor_rotate(): pl.pallas_call(fac_kernel, out_shape=jax.ShapeDtypeStruct((8, B, B), BF),...  119 us
    pallas_call x1, Pallas kernels, total(): pl.pallas_call(sum_kernel, out_shape=jax.ShapeDtypeStruct((2, 9216, 128),...  69.4 us
    pallas_call x1, Pallas kernels, swap(): pl.pallas_call(swap_kernel, out_shape=jax.ShapeDtypeStruct((2, 8, 256, 25...  22.6 us
    pallas_call x1, Pallas kernels, gram(): pl.pallas_call(gram_kernel, out_shape=jax.ShapeDtypeStruct((9216, 128), X...  7.02 us
    unnamed x8, local copies, waits for them, and re-layouts  6.21 us

profile of v2, /device:TPU:1, one launch (start us, length us, event | category | flops | bytes accessed | tf_op | source)
XLA Modules:
  0.0 233.3 jit_solution(11871363586380367746)
XLA Ops:
  0.0 0.0 copy-start
  0.0 0.7 broadcast_compare_fusion.1
  0.7 0.1 convert_reduce_fusion
  0.8 0.7 broadcast_select_fusion
  1.5 0.8 select_reduce_fusion
  2.3 0.1 broadcast_in_dim.75
  2.4 0.1 eq.58
  2.5 0.1 broadcast_compare_fusion
  2.6 0.0 copy-done
  2.6 0.3 fusion.1
  2.9 0.2 broadcast_in_dim.76
  3.1 0.1 broadcast_in_dim.77
  3.2 0.1 broadcast_multiply_fusion
  3.3 0.1 mul.24.cb_ref
  3.5 1.0 copy.26
  4.5 0.2 copy.16
  4.6 0.2 convolution_select_fusion
  4.9 22.6 %shard_map.82.x_ref = bf16[2,8,256,256]{3,2,1,0:T(8,128)(2,1)} custom-call(bf16[2048,256]{1,0:T(8,128)(2,1)} %x_ref.1), custom_call_target="tpu_custom_call" | custom-call | tf_op jit(solution)/shard_map/pallas_call | solution.py:168
  27.5 2.3 dynamic-slice_bitcast_fusion.x_ref
  29.8 0.0 copy-start.2
  29.8 1.6 copy-done.2
  31.4 7.0 %shard_map.83.p_ref = f32[9216,128]{1,0:T(8,128)S(1)} custom-call(s32[18]{0:T(128)S(1)} %get-tuple-element.8.p_tab, s32[18]{0:T(128)S(1)} %get-tuple-element.7.q_tab, bf16[2,8,256,256]{3,2,1,0:T(8,128)(2,1)S(1)} %copy-done.2, bf16[2,64,256]{2,1,0:T(8,128)(2,1)S(1)} %select_convert_fusion.pm_ref, f32[64,64]{1,0:T(8,128)S(1)} %mul.24.cb_ref), custom_call_target="tpu_custom_call" | custom-call | tf_op jit(solution)/shard_map/pallas_call | solution.py:204
  38.4 69.4 %shard_map.84.m_ref = f32[2,9216,128]{2,1,0:T(8,128)S(1)} custom-call(f32[9216,128]{1,0:T(8,128)S(1)} %shard_map.83.p_ref), custom_call_target="tpu_custom_call" | custom-call | tf_op jit(solution)/shard_map/pallas_call | solution.py:314
  107.8 0.0 copy-start.1
  107.8 3.6 %copy-done.1 = f32[2,9216,128]{2,1,0:T(8,128)} copy-done((f32[2,9216,128]{2,1,0:T(8,128)}, f32[2,9216,128]{2,1,0:T(8,128)S(1)}, u32[]{:S(2)}) %copy-start.1) | copy-done | bytes 9437208
  111.4 119.0 %shard_map.85 = bf16[8,256,256]{2,1,0:T(8,128)(2,1)} custom-call(f32[2,9216,128]{2,1,0:T(8,128)} %copy-done.1, bf16[8,256,256]{2,1,0:T(8,128)(2,1)} %dynamic-slice_bitcast_fusion.x_ref), custom_call_target="tpu_custom_call" | custom-call | tf_op jit(solution)/shard_map/pallas_call | solution.py:107
  230.4 1.5 copy.19
  231.9 1.4 copy.20
  (9 shorter events, 0.1 us)
Async XLA Ops:
  0.0 2.6 %copy-start = (f32[128,8,8]{0,2,1:T(8,128)S(1)}, f32[128,8,8]{0,2,1:T(8,128)}, u32[]{:S(2)}) copy-start(f32[128,8,8]{0,2,1:T(8,128)} %param.13) | copy-start | bytes 98308
  29.8 1.6 copy-start.2
  107.8 3.6 %copy-start.1 = (f32[2,9216,128]{2,1,0:T(8,128)}, f32[2,9216,128]{2,1,0:T(8,128)S(1)}, u32[]{:S(2)}) copy-start(f32[2,9216,128]{2,1,0:T(8,128)S(1)} %shard_map.84.m_ref) | copy-start | bytes 28311556

commit v3 on v2

--- a/solution.py
+++ b/solution.py
@@ -12,105 +12,135 @@
 A_SLAB = 8
 
 
-def chol_inv_128(a_ref, w_ref):
-    n=128; T=16
+def chol_inv_128(a_ref, w_ref, extra=None):
+    T=16
+    full=(8,128)
+    lane=lax.broadcasted_iota(jnp.int32,full,1)
+    sub=lax.broadcasted_iota(jnp.int32,full,0)
+    spread=lambda v,k: jnp.broadcast_to(v[:,k:k+1],full)
+    row=lambda v,c: jnp.broadcast_to(v[c:c+1,:],full)
     A=[a_ref[8*t:8*t+8,:] for t in range(T)]
-    lane=lax.broadcasted_iota(jnp.int32,(8,128),1)
-    sub=lax.broadcasted_iota(jnp.int32,(8,128),0)
     W=[jnp.where(lane==sub+8*t,1.0,0.0).astype(F32) for t in range(T)]
+    zero=jnp.minimum(jnp.abs(A[0]),0.0)
+    D=[spread(A[0],c)+zero for c in range(8)]
     for g in range(T):
-        C=[[jnp.broadcast_to(A[t][:,8*g+c:8*g+c+1],(8,128)) for t in range(T)] if True else None for c in range(0)]
-        C=[{t:jnp.broadcast_to(A[t][:,8*g+c:8*g+c+1],(8,128)) for t in range(g,T)} for c in range(8)]
-        S=jnp.ones((8,128),F32)
+        C={t:[spread(A[t],8*g+c) for c in range(8)] for t in range(g+1,T)}
+        if g+1<T:
+            N=[spread(A[g+1],8*g+8+c) for c in range(8)]
+        inv=[];ra=[];rw=[];rc=[]
+        S=jnp.ones(full,F32)
         for c in range(8):
-            d=jnp.broadcast_to(C[c][g][c:c+1,:],(8,128))
+            d=row(D[c],c)
             S=jnp.where(sub==c,d,S)
-            inv=1.0/d
-            Cc=dict(C[c])
+            inv.append(1.0/d)
+            ra.append(row(A[g],c)*inv[c])
+            rw.append(row(W[g],c)*inv[c])
+            rc.append({j:row(D[j],c)*inv[c] for j in range(c+1,8)})
             if c<7:
-                Cc[g]=jnp.where(sub>c,C[c][g],0.0)
-            ra=jnp.broadcast_to(A[g][c:c+1,:],(8,128))*inv
-            rw=jnp.broadcast_to(W[g][c:c+1,:],(8,128))*inv
-            rc={j:jnp.broadcast_to(C[j][g][c:c+1,:],(8,128))*inv for j in range(c+1,8)}
-            t0=g if c<7 else g+1
-            for t in range(t0,T):
+                m=jnp.where(sub>c,D[c],0.0)
                 for j in range(c+1,8):
-                    C[j][t]=C[j][t]-Cc[t]*rc[j]
-                A[t]=A[t]-Cc[t]*ra
-                W[t]=W[t]-Cc[t]*rw
+                    D[j]=D[j]-m*rc[c][j]
+                A[g]=A[g]-m*ra[c]
+                W[g]=W[g]-m*rw[c]
         w_ref[8*g:8*g+8,:]=W[g]*lax.rsqrt(S)
-
-
+        if extra is not None: extra(g)
+        for t in range(g+1,T):
+            for c in range(8):
+                for j in range(c+1,8):
+                    C[t][j]=C[t][j]-C[t][c]*rc[c][j]
+                A[t]=A[t]-C[t][c]*ra[c]
+                W[t]=W[t]-C[t][c]*rw[c]
+            if t==g+1:
+                for c in range(8):
+                    e=C[t][c]*inv[c]
+                    for k in range(8):
+                        N[k]=N[k]-C[t][c]*row(e,k)
+                D=N
+
+
+PAIRS = [(i, c) for i in range(8) for c in range(i, 8)]
+HI=lax.Precision.HIGHEST
 B=256
-HI=lax.Precision.HIGHEST
 def splt(x):
     h=x.astype(BF); return h,(x-h.astype(F32)).astype(BF)
 def nt(a,b,prec=None):
     return lax.dot_general(a,b,(((1,),(1,)),((),())),preferred_element_type=F32,precision=prec)
-def tn(a,b,prec=None):
-    return lax.dot_general(a,b,(((0,),(0,)),((),())),preferred_element_type=F32,precision=prec)
 def nn(a,b,prec=None):
     return lax.dot_general(a,b,(((1,),(0,)),((),())),preferred_element_type=F32,precision=prec)
-
-def fac_kernel(m_ref, x_ref, o_ref, T, UT, U, Wd, Ws, Wt, sem):
-    NBK=8
-    cps=[]
-    for i in range(NBK):
-        for c in range(i,NBK):
-            t=PAIRS.index((i,c))
-            for h in range(2):
-                k=len(cps)
-                cp=pltpu.make_async_copy(m_ref.at[t//18,pl.ds((t%18)*512+256*h,256),:],T.at[i,c,:,pl.ds(128*h,128)],sem.at[k])
-                cp.start(); cps.append(cp)
+def left(x):
+    h,l=splt(x); return jnp.concatenate([h,h,l],axis=1)
+def right(x):
+    h,l=splt(x); return jnp.concatenate([h,l,h],axis=0)
+
+NBK=8
+def later_tiles():
+    rows,cols=[],[]
+    for j in range(NBK):
+        todo=[(i,c) for i in range(j+1,NBK) for c in range(i,NBK)]+[(8,c) for c in range(j+1,NBK)] if j else []
+        assert len(todo)<=32
+        todo=todo+[(7,0)]*(32-len(todo))
+        rows+=[i for i,_ in todo]; cols+=[c for _,c in todo]
+    return rows,cols
+
+def fac_kernel(core_ref, ti_ref, tc_ref, m_ref, x_ref, o_ref, T, UT, U, Wd, Ws, Wt):
+    core=core_ref[0]
+    for t,(i,c) in enumerate(PAIRS):
+        for h in range(2):
+            T[i,c,:,128*h:128*h+128]=m_ref[t//18,(t%18)*512+256*h:(t%18)*512+256*h+256,:].astype(F32)
     for c in range(NBK):
-        T[8,c]=x_ref[c].astype(F32)
-    for cp in cps: cp.wait()
+        T[8,c]=x_ref[core,c].astype(F32)
     Wd[...]=jnp.zeros((B,B),F32)
+    UT[7]=jnp.zeros((B,3*B),BF); U[0]=jnp.zeros((3*B,B),BF); T[7,0]=jnp.zeros((B,B),F32)
+    def tile(i,c):
+        T[i,c]=T[i,c]-nn(UT[i],U[c])
     def step(j,_):
+        def slot(s):
+            k=j*32+s
+            tile(ti_ref[k],tc_ref[k])
         D=T.at[j,j]
-        chol_inv_128(D.at[pl.ds(0,128),pl.ds(0,128)],Wd.at[pl.ds(0,128),pl.ds(0,128)])
+        chol_inv_128(D.at[pl.ds(0,128),pl.ds(0,128)],Wd.at[pl.ds(0,128),pl.ds(0,128)],lambda g: slot(g))
         W1=Wd[0:128,0:128]
-        u12=nn(W1,T[j,j,0:128,128:256],HI)
-        T[j,j,128:256,128:256]=T[j,j,128:256,128:256]-tn(u12,u12,HI)
-        chol_inv_128(D.at[pl.ds(128,128),pl.ds(128,128)],Wd.at[pl.ds(128,128),pl.ds(128,128)])
+        u12=nn(left(W1),right(T[j,j,0:128,128:256]))
+        l21=left(u12.T)
+        T[j,j,128:256,128:256]=T[j,j,128:256,128:256]-nn(l21,right(u12))
+        V=nn(l21,right(W1))
+        chol_inv_128(D.at[pl.ds(128,128),pl.ds(128,128)],Wd.at[pl.ds(128,128),pl.ds(128,128)],lambda g: slot(16+g))
         W2=Wd[128:256,128:256]
-        Wd[128:256,0:128]=-nn(W2,tn(u12,W1,HI),HI)
+        Wd[128:256,0:128]=-nn(left(W2),right(V))
         h,l=splt(Wd[...])
         Ws[:,0:B]=h; Ws[:,B:2*B]=h; Ws[:,2*B:3*B]=l
         Wt[:,0:B]=h; Wt[:,B:2*B]=l; Wt[:,2*B:3*B]=h
-        h,l=splt(T[8,j])
-        r=nt(jnp.concatenate([h,h,l],axis=1),Wt[...])
+        r=nt(left(T[8,j]),Wt[...])
         h=r.astype(BF)
-        o_ref[j]=h
+        o_ref[:,pl.ds(pl.multiple_of(j*B,B),B)]=h
         l=(r-h.astype(F32)).astype(BF)
         UT[8,:,0:B]=h; UT[8,:,B:2*B]=h; UT[8,:,2*B:3*B]=l
         def pan(c,_):
-            h,l=splt(T[j,c])
-            u=nn(Ws[...],jnp.concatenate([h,l,h],axis=0))
+            u=nn(Ws[...],right(T[j,c]))
             h,l=splt(u)
             U[c,0:B,:]=h; U[c,B:2*B,:]=l; U[c,2*B:3*B,:]=h
-            h,l=splt(u.T)
-            UT[c,:,0:B]=h; UT[c,:,B:2*B]=h; UT[c,:,2*B:3*B]=l
+            UT[c]=left(u.T)
             return 0
         lax.fori_loop(j+1,NBK,pan,0)
-        def row(i,_):
-            def col(c,_):
-                T[i,c]=T[i,c]-nn(UT[i],U[c])
-                return 0
-            lax.fori_loop(jnp.where(i==8,j+1,i),NBK,col,0)
+        def urgent(c,_):
+            tile(j+1,c)
             return 0
-        lax.fori_loop(j+1,NBK+1,row,0)
+        lax.fori_loop(j+1,NBK,urgent,0)
+        @pl.when(j<NBK-1)
+        def _():
+            tile(8,j+1)
         return 0
     lax.fori_loop(0,NBK,step,0)
 
-def factor_rotate(metric, mine):
-    o=pl.pallas_call(fac_kernel,out_shape=jax.ShapeDtypeStruct((8,B,B),BF),
-      in_specs=[pl.BlockSpec(memory_space=pltpu.HBM),pl.BlockSpec(memory_space=pltpu.VMEM)],
-      out_specs=pl.BlockSpec(memory_space=pltpu.VMEM),
+def factor_rotate(core, metric, rows):
+    vm=pl.BlockSpec(memory_space=pltpu.VMEM); sm=pl.BlockSpec(memory_space=pltpu.SMEM)
+    ti,tc=later_tiles()
+    return pl.pallas_call(fac_kernel,out_shape=jax.ShapeDtypeStruct((B,8*B),BF),
+      in_specs=[sm,sm,sm,vm,vm], out_specs=vm,
       scratch_shapes=[pltpu.VMEM((9,8,B,B),F32),pltpu.VMEM((9,B,3*B),BF),pltpu.VMEM((8,3*B,B),BF),
-         pltpu.VMEM((B,B),F32),pltpu.VMEM((B,3*B),BF),pltpu.VMEM((B,3*B),BF),pltpu.SemaphoreType.DMA((72,))],
-      compiler_params=pltpu.CompilerParams(vmem_limit_bytes=56*2**20))(metric,mine)
-    return o.transpose(1,0,2).reshape(B,8*B)
+         pltpu.VMEM((B,B),F32),pltpu.VMEM((B,3*B),BF),pltpu.VMEM((B,3*B),BF)],
+      compiler_params=pltpu.CompilerParams(vmem_limit_bytes=56*2**20))(
+        core.reshape(1),jnp.asarray(ti,jnp.int32),jnp.asarray(tc,jnp.int32),metric,rows)
 
 
 MESH = pl.DeviceIdType.MESH
@@ -323,9 +353,6 @@
                                              vmem_limit_bytes=40 * 2**20))(part)
 
 
-PAIRS = [(i, c) for i in range(8) for c in range(i, 8)]
-
-
 def shards(orbitals, projectors, sphere_start, proj_count, owner_slab, correlation_coef):
     band = lax.axis_index("band")
     slab = lax.axis_index("grid")
@@ -353,8 +380,7 @@
     rows = swap(orbitals)
     part = gram(p_tab, q_tab, rows, pm, cb)
     metric = total(part)
-    mine = lax.dynamic_index_in_dim(rows, core, 0, keepdims=False)
-    return factor_rotate(metric, mine)
+    return factor_rotate(core, metric, rows)
 
 
 def solution(mesh):

time: 234 us -> 193 us (0.82)
  Pallas kernels: 218 us -> 183 us
  local copies, waits for them, and re-layouts: 12.2 us -> 7.02 us
    pallas_call x1, Pallas kernels: 119 us -> 83.8 us  [factor_rotate(): pl.pallas_call(fac_kernel, out_shape=jax.ShapeDtypeStruct((B, 8 * B), BF)...]
where the time goes in v3:
time: 193 us
  Pallas kernels  183 us (95%)
  local copies, waits for them, and re-layouts  7.02 us (4%)
  other arithmetic  2.5 us (1%)
    pallas_call x1, Pallas kernels, factor_rotate(): pl.pallas_call(fac_kernel, out_shape=jax.ShapeDtypeStruct((B, 8 * B), BF)...  83.8 us
    pallas_call x1, Pallas kernels, total(): pl.pallas_call(sum_kernel, out_shape=jax.ShapeDtypeStruct((2, 9216, 128),...  69.4 us
    pallas_call x1, Pallas kernels, swap(): pl.pallas_call(swap_kernel, out_shape=jax.ShapeDtypeStruct((2, 8, 256, 25...  22.6 us
    pallas_call x1, Pallas kernels, gram(): pl.pallas_call(gram_kernel, out_shape=jax.ShapeDtypeStruct((9216, 128), X...  7.02 us
    unnamed x8, local copies, waits for them, and re-layouts  6.21 us

profile of v3, /device:TPU:1, one launch (start us, length us, event | category | flops | bytes accessed | tf_op | source)
XLA Modules:
  0.0 192.9 jit_solution(16275130334160741059)
XLA Ops:
  0.0 0.0 copy-start
  0.0 0.7 broadcast_compare_fusion.1
  0.7 0.1 convert_reduce_fusion
  0.8 0.7 broadcast_select_fusion
  1.5 0.8 select_reduce_fusion
  2.3 0.1 broadcast_in_dim.75
  2.4 0.1 eq.58
  2.5 0.1 broadcast_compare_fusion
  2.6 0.0 copy-done
  2.6 0.3 fusion.1
  2.9 0.2 broadcast_in_dim.76
  3.1 0.1 broadcast_in_dim.77
  3.2 0.1 broadcast_multiply_fusion
  3.3 0.1 mul.24.cb_ref
  3.5 1.0 copy.24
  4.5 0.2 copy.16
  4.6 0.2 convolution_select_fusion
  4.9 22.6 %shard_map.100.x_ref = bf16[2,8,256,256]{3,2,1,0:T(8,128)(2,1)} custom-call(bf16[2048,256]{1,0:T(8,128)(2,1)} %x_ref.1), custom_call_target="tpu_custom_call" | custom-call | tf_op jit(solution)/shard_map/pallas_call | solution.py:198
  27.5 0.0 copy-start.2
  27.5 1.6 copy-done.2
  29.1 7.0 %shard_map.101.p_ref = f32[9216,128]{1,0:T(8,128)S(1)} custom-call(s32[18]{0:T(128)S(1)} %get-tuple-element.8.p_tab, s32[18]{0:T(128)S(1)} %get-tuple-element.7.q_tab, bf16[2,8,256,256]{3,2,1,0:T(8,128)(2,1)S(1)} %copy-done.2, bf16[2,64,256]{2,1,0:T(8,128)(2,1)S(1)} %select_convert_fusion.pm_ref, f32[64,64]{1,0:T(8,128)S(1)} %mul.24.cb_ref), custom_call_target="tpu_custom_call" | custom-call | tf_op jit(solution)/shard_map/pallas_call | solution.py:234
  36.1 69.4 %shard_map.102.m_ref = f32[2,9216,128]{2,1,0:T(8,128)S(1)} custom-call(f32[9216,128]{1,0:T(8,128)S(1)} %shard_map.101.p_ref), custom_call_target="tpu_custom_call" | custom-call | tf_op jit(solution)/shard_map/pallas_call | solution.py:344
  105.5 0.0 copy-start.1
  105.5 3.6 %copy-done.1 = f32[2,9216,128]{2,1,0:T(8,128)} copy-done((f32[2,9216,128]{2,1,0:T(8,128)}, f32[2,9216,128]{2,1,0:T(8,128)S(1)}, u32[]{:S(2)}) %copy-start.1) | copy-done | bytes 9437208
  109.1 83.8 %shard_map.103 = bf16[256,2048]{1,0:T(8,128)(2,1)} custom-call(s32[1]{0:T(128)} %bitcast.core_ref, s32[256]{0:T(256)} %constant.64.clone.ti_ref, s32[256]{0:T(256)} %constant.65.clone.tc_ref, f32[2,9216,128]{2,1,0:T(8,128)} %copy-done.1, bf16[2,8,256,256]{3,2,1,0:T(8,128)(2,1)} %shard_map.100.x_ref), custom_call_target="tpu_custom_call" | custom-call | tf_op jit(solution)/shard_map/pallas_call | solution.py:138
  (9 shorter events, 0.1 us)
Async XLA Ops:
  0.0 2.6 %copy-start = (f32[128,8,8]{0,2,1:T(8,128)S(1)}, f32[128,8,8]{0,2,1:T(8,128)}, u32[]{:S(2)}) copy-start(f32[128,8,8]{0,2,1:T(8,128)} %param.15) | copy-start | bytes 98308
  27.5 1.6 copy-start.2
  105.5 3.6 %copy-start.1 = (f32[2,9216,128]{2,1,0:T(8,128)}, f32[2,9216,128]{2,1,0:T(8,128)S(1)}, u32[]{:S(2)}) copy-start(f32[2,9216,128]{2,1,0:T(8,128)S(1)} %shard_map.102.m_ref) | copy-start | bytes 28311556
